TPU v7x, 32 devices: a whole 2x2x4 slice. The times are simulated.
32 devices in a mesh: seq: 8 (over z, y), head: 4 (over x, core).
Axes of the slice: x: 2, y: 2, z: 4, core: 2. Of those that a mesh axis runs over, the one named last changes fastest.
Arguments:
- queries: bfloat16 [2048, 2048], P(('seq', 'head')), may hold values from -200 to 200
- keys: bfloat16 [2048, 2048], P(('seq', 'head')), may hold values from -15 to 15
- values: bfloat16 [2048, 2048], P(('seq', 'head')), may hold values from -6 to 6
- random_blocks: int32 [32, 16, 3], P('seq', 'head'), may hold values from 0 to 31, as said below
- global_blocks: int32 [2], replicated, may hold values from 0 to 31, as said below
Outputs:
- attention: float32 [2048, 2048], P('seq', 'head')
Inputs may be any that keep to these rules, and one draw needn't show every extreme that they name: `random_blocks`: over the 4 query blocks and 4 heads of one device (one index of seq and one of head), at most 9 entries name blocks of any one shard of 4 consecutive blocks; in every draw some device names exactly 9 blocks of one shard. Entries may repeat and may fall on the window or on a global block. `global_blocks`: two different block numbers; one of them is 31.
All inputs are finite; a program needn't handle non-finite values.
Results may differ from a plain program's by a relative error of at most 0.0023.
Values may be sent and summed in bfloat16 or wider, within the bound.
A program may use at most 128 MiB of HBM per device.

v0:
```python
import functools
import math

import jax
import jax.numpy as jnp
from jax import lax
from jax.experimental import pallas as pl
from jax.experimental.pallas import tpu as pltpu
from jax.sharding import PartitionSpec as P

HEAD_DIM = 128
BLK = 64


MASKED = -1e30


def extended(block, sides, width):
    for axis, dim in sides:
        count = lax.axis_size(axis)
        forward = [(i, i + 1) for i in range(count - 1)]
        backward = [(target, source) for source, target in forward]
        low = lax.ppermute(
            lax.slice_in_dim(block, block.shape[dim] - width, None, axis=dim), axis, forward
        )
        high = lax.ppermute(lax.slice_in_dim(block, 0, width, axis=dim), axis, backward)
        block = jnp.concatenate([low, block, high], axis=dim)
    return block


def combined_all(value, axis, join):
    pieces = jax.tree.map(lambda part: lax.all_gather(part, axis), value)
    head = jax.tree.map(lambda part: part[0], pieces)
    tail = jax.tree.map(lambda part: part[1:], pieces)
    so_far, _ = lax.scan(lambda so_far, slab: (join(so_far, slab), None), head, tail)
    return so_far


def merge_parts(former, latter):
    peaks = jnp.maximum(former[0], latter[0])
    former_fade = jnp.exp(former[0] - peaks)
    latter_fade = jnp.exp(latter[0] - peaks)
    return (
        peaks,
        former[1] * former_fade + latter[1] * latter_fade,
        former[2] * former_fade[..., None] + latter[2] * latter_fade[..., None],
    )


def soft_parts(scores):
    peaks = jnp.max(scores, axis=(-2, -1))
    powers = jnp.exp(scores - peaks[..., None, None])
    return (peaks, jnp.sum(powers, axis=(-2, -1)), powers.astype(jnp.bfloat16))


def make_requests(rand_lists, seq_count, capacity):
    blk_dev, heads_dev, rand_count = rand_lists.shape
    flat_list = rand_lists.reshape(-1)
    owners = flat_list // blk_dev
    head_ids = jnp.broadcast_to(
        jnp.arange(heads_dev, dtype=jnp.int32)[None, :, None], rand_lists.shape
    ).reshape(-1)
    item_ids = flat_list % blk_dev * heads_dev + head_ids
    position = jnp.arange(flat_list.shape[0], dtype=jnp.int32)
    earlier = (owners[:, None] == owners[None, :]) & (position[None, :] < position[:, None])
    slot_ids = owners * capacity + jnp.sum(earlier.astype(jnp.int32), axis=1)
    requests = jnp.zeros((seq_count * capacity,), jnp.int32).at[slot_ids].set(item_ids)
    sources = jnp.zeros((seq_count * capacity,), jnp.int32).at[slot_ids].set(position)
    return (requests.reshape(seq_count, capacity), slot_ids, sources)


def exchanged(queries, keys, values, random_blocks, global_blocks):
    seq_count = lax.axis_size("seq")
    seq_index = lax.axis_index("seq")
    query_rows, key_rows, value_rows = (
        lax.all_to_all(queries, "head", split_axis=1, concat_axis=0, tiled=True),
        lax.all_to_all(keys, "head", split_axis=1, concat_axis=0, tiled=True),
        lax.all_to_all(values, "head", split_axis=1, concat_axis=0, tiled=True),
    )
    tokens = query_rows.shape[0]
    blk_dev = tokens // BLK
    heads_dev = query_rows.shape[1] // HEAD_DIM
    rand_count = random_blocks.shape[2]
    glob_count = global_blocks.shape[0]
    total_blocks = blk_dev * seq_count
    first_block = seq_index * blk_dev
    capacity = (blk_dev * heads_dev * rand_count * 3 // 2 + seq_count - 1) // seq_count
    score_scale = 1.0 / math.sqrt(HEAD_DIM)
    shape_four = (blk_dev, BLK, heads_dev, HEAD_DIM)
    query_four = query_rows.reshape(shape_four)
    key_four = key_rows.reshape(shape_four)
    value_four = value_rows.reshape(shape_four)
    paired = jnp.stack([key_rows, value_rows])
    padded = extended(paired, (("seq", 1),), BLK)
    padded = padded.reshape(2, blk_dev + 2, BLK, heads_dev, HEAD_DIM)
    window = jnp.stack([padded[:, offset : offset + blk_dev] for offset in range(3)], axis=2)
    near_ids = (
        first_block
        + jnp.arange(blk_dev, dtype=jnp.int32)[:, None]
        + jnp.arange(-1, 2, dtype=jnp.int32)[None, :]
    )
    inside = (near_ids >= 0) & (near_ids < total_blocks)
    stacked = jnp.stack([query_rows, key_rows, value_rows]).reshape(
        3, blk_dev, BLK, heads_dev * HEAD_DIM
    )
    owned_mask = global_blocks // blk_dev == seq_index
    local_ids = jnp.where(owned_mask, global_blocks - first_block, 0)
    picked = (
        jnp.take(stacked, local_ids, axis=1).astype(jnp.float32)
        * owned_mask.astype(jnp.float32)[None, :, None, None]
    )
    glob_rows = lax.psum(picked, "seq").astype(jnp.bfloat16)
    glob_rows = glob_rows.reshape(3, glob_count, BLK, heads_dev, HEAD_DIM)
    requests, slot_ids, sources = make_requests(random_blocks, seq_count, capacity)
    incoming = lax.all_to_all(requests, "seq", split_axis=0, concat_axis=0, tiled=True)

    def by_block(row_data):
        return (
            row_data.reshape(shape_four)
            .transpose(0, 2, 1, 3)
            .reshape(blk_dev * heads_dev, BLK, HEAD_DIM)
        )

    pair_blocks = jnp.stack([by_block(key_rows), by_block(value_rows)], axis=1)
    served = pair_blocks[incoming]
    key_win, value_win = (window[0], window[1])
    win_scores = (
        jnp.einsum("jqhd,jwkhd->jhqwk", query_four, key_win, preferred_element_type=jnp.float32)
        * score_scale
    )
    win_scores = jnp.where(inside[:, None, None, :, None], win_scores, MASKED)
    glob_scores = (
        jnp.einsum("jqhd,gkhd->jhqgk", query_four, glob_rows[1], preferred_element_type=jnp.float32)
        * score_scale
    )
    split_at = 3 + glob_count
    arrived_pairs = lax.all_to_all(served, "seq", split_axis=0, concat_axis=0, tiled=True)
    tail = arrived_pairs.shape[2:]
    rand_pairs = arrived_pairs.reshape((seq_count * capacity,) + tail)[slot_ids].reshape(
        (blk_dev, heads_dev, rand_count) + tail
    )
    rand_scores = (
        jnp.einsum(
            "jqhd,jhrkd->jhqrk",
            query_four,
            rand_pairs[:, :, :, 0],
            preferred_element_type=jnp.float32,
        )
        * score_scale
    )
    peaks, totals, weights = soft_parts(
        jnp.concatenate([win_scores, glob_scores, rand_scores], axis=3)
    )
    sums_all = jnp.einsum(
        "jhqwk,jwkhd->jhqd", weights[:, :, :, 0:3], value_win, preferred_element_type=jnp.float32
    )
    sums_all = sums_all + jnp.einsum(
        "jhqgk,gkhd->jhqd",
        weights[:, :, :, 3:split_at],
        glob_rows[2],
        preferred_element_type=jnp.float32,
    )
    sums_all = sums_all + jnp.einsum(
        "jhqrk,jhrkd->jhqd",
        weights[:, :, :, split_at:],
        rand_pairs[:, :, :, 1],
        preferred_element_type=jnp.float32,
    )
    running = (peaks, totals, sums_all)
    sparse_out = (running[2] / running[1][..., None]).transpose(0, 2, 1, 3)
    full_scores = (
        jnp.einsum("gqhd,jkhd->hgqjk", glob_rows[0], key_four, preferred_element_type=jnp.float32)
        * score_scale
    )
    full_peaks, full_totals, full_weights = soft_parts(full_scores)
    full_sum = jnp.einsum(
        "hgqjk,jkhd->hgqd", full_weights, value_four, preferred_element_type=jnp.float32
    )
    merged = combined_all((full_peaks, full_totals, full_sum), "seq", merge_parts)
    glob_out = (merged[2] / merged[1][..., None]).transpose(1, 2, 0, 3)
    block_ids = first_block + jnp.arange(blk_dev, dtype=jnp.int32)
    result = sparse_out
    for glob_id in range(glob_count):
        matches = (block_ids == global_blocks[glob_id])[:, None, None, None]
        result = jnp.where(matches, glob_out[glob_id][None], result)
    return result.reshape(tokens, heads_dev * HEAD_DIM)


GATHER_LIMIT = 16 * 2**20


def gathered_kernel(
    seq_count, head_count, rand_count, glob_count,
    q_hbm, k_hbm, v_hbm, rand_ref, glob_ref, out_ref,
    pool, rand_vmem, q_all, stage, q_stage, listed, peak_ref, total_ref, acc_ref,
    local_sem, send_sem, recv_sem, q_recv_sem,
):
    seq = lax.axis_index("seq")
    head = lax.axis_index("head")
    depth = seq_count // 2
    z, y = seq // 2, seq % 2
    rows, width = q_all.shape[1], q_all.shape[2]
    heads_dev = width // HEAD_DIM
    tokens = head_count * rows
    classes = head_count

    def lane(k):
        return ((head // 2 + k // 2) % (head_count // 2)) * 2 + (head % 2 + k % 2) % 2

    def shard(dz, dy):
        return ((z + dz) % depth) * 2 + (y + dy) % 2

    def spot(dz, dy, k):
        return shard(dz, dy) * head_count + lane(k)

    names_copy = pltpu.make_async_copy(rand_ref, rand_vmem, local_sem.at[3 * classes])
    names_copy.start()
    loads = []
    for k in range(classes):
        cols = pl.ds(pl.multiple_of(lane(k) * width, 128), width)
        target = pool.at[spot(0, 0, 0)] if k == 0 else stage.at[k - 1]
        q_target = q_all.at[head] if k == 0 else q_stage.at[k - 1]
        trio = []
        for n, (source, dest) in enumerate(
            ((k_hbm, target.at[0]), (v_hbm, target.at[1]), (q_hbm, q_target))
        ):
            trio.append(pltpu.make_async_copy(source.at[:, cols], dest, local_sem.at[k * 3 + n]))
        loads.append(trio)
    for trio in loads:
        trio[0].start()
        trio[1].start()
    for trio in loads:
        trio[2].start()

    barrier = pltpu.get_barrier_semaphore()
    friends = [{"seq": seq, "head": lane(k)} for k in range(1, classes)]
    friends.append({"seq": shard(0, 1), "head": head})
    up = {"seq": shard(1, 0), "head": head}
    down = {"seq": shard(-1, 0), "head": head}
    across = {"seq": shard(0, 1), "head": head}

    def greet(friend):
        pl.semaphore_signal(barrier, inc=1, device_id=friend, device_id_type=pl.DeviceIdType.MESH)

    for friend in friends:
        greet(friend)
    pl.when(z < depth - 1)(lambda: greet(up))
    pl.when(z > 0)(lambda: greet(down))
    names_copy.wait()

    query_block = seq * (tokens // BLK) + lax.broadcasted_iota(jnp.int32, (1, tokens), 1) // BLK
    local_block = lax.broadcasted_iota(jnp.int32, (1, tokens), 1) // BLK
    for hd in range(heads_dev):
        for r in range(rand_count):
            names = jnp.zeros((1, tokens), jnp.int32)
            for b in range(tokens // BLK):
                names = jnp.where(local_block == b, rand_vmem[b, pl.ds(hd, 1), pl.ds(r, 1)], names)
            listed[pl.ds(hd * rand_count + r, 1), :] = names
    is_glob = query_block == glob_ref[0]
    for g in range(1, glob_count):
        is_glob = is_glob | (query_block == glob_ref[g])
    glob_row = jnp.where(is_glob, 1, 0)
    peak_ref[...] = jnp.full_like(peak_ref, MASKED)
    total_ref[...] = jnp.zeros_like(total_ref)
    acc_ref[...] = jnp.zeros_like(acc_ref)

    for trio in loads:
        trio[0].wait()
        trio[1].wait()
    for trio in loads:
        trio[2].wait()
    line_friends = (z + depth - 1) // depth + (2 * depth - 2 - z) // depth
    pl.semaphore_wait(barrier, len(friends) + line_friends)

    pending = []
    landed = {(0, 0, 0, 2)}
    everywhere = z >= 0
    cuts = [(2,)] * (classes - 1) + [(0, 1)]
    y_first = {(classes - 1, 0)}

    def remote(source, dest, sender, receiver, device):
        return pltpu.make_async_remote_copy(
            src_ref=source, dst_ref=dest, send_sem=sender, recv_sem=receiver,
            device_id=device, device_id_type=pl.DeviceIdType.MESH,
        )

    def view(ref, place, cut):
        return ref.at[place] if cut == 2 else ref.at[place, cut]

    def post(source, dest, receiver, device, when=everywhere):
        sender = send_sem.at[len(pending)]
        pl.when(when)(lambda: remote(source, dest, sender, receiver, device).start())
        pending.append((source, dest, sender, receiver, device, when))

    def push(dz, dy, k, cut, device, when=everywhere):
        place = spot(dz, dy, k)
        piece = view(pool, place, cut)
        post(piece, piece, recv_sem.at[place, cut % 2], device, when)

    def exists(dz):
        return z >= -dz if dz < 0 else z + dz < depth

    def arrive(dz, dy, k, cut, when=everywhere):
        key = (dz, dy, k, cut)
        if key in landed:
            return
        landed.add(key)
        place = spot(dz, dy, k)
        piece = view(pool, place, cut)
        pl.when(when)(
            lambda: remote(
                piece, piece, send_sem.at[0], recv_sem.at[place, cut % 2], across
            ).wait_recv()
        )

    others = list(range(2, classes)) + [1]
    mine = seq * head_count + head
    for k in others:
        for cut in cuts[k]:
            post(
                view(stage, k - 1, cut), view(pool, mine, cut), recv_sem.at[mine, cut % 2],
                {"seq": seq, "head": lane(k)},
            )

    def own(k):
        for cut in cuts[k]:
            arrive(0, 0, k, cut)
            push(0, 0, k, cut, across)
            push(0, 0, k, cut, up, z < depth - 1)
            push(0, 0, k, cut, down, z > 0)

    def onward(dz, dy, k, cut, cross):
        here = exists(dz)
        arrive(dz, dy, k, cut, here)
        if dz < 0 and -dz < depth - 1:
            push(dz, dy, k, cut, up, here & (z < depth - 1))
        if dz > 0 and dz < depth - 1:
            push(dz, dy, k, cut, down, here & (z > 0))
        if cross:
            push(dz, dy, k, cut, across, here)

    def hop(k, t):
        for cut in cuts[k]:
            early = (k, cut) in y_first
            for dz in (-t, t):
                onward(dz, 0, k, cut, not early)

    def partner_hop(t):
        for k, cut in sorted(y_first):
            for dz in (-t, t):
                onward(dz, 1, k, cut, False)

    def partner():
        for k, cut in sorted(y_first):
            arrive(0, 1, k, cut)
            push(0, 1, k, cut, up, z < depth - 1)
            push(0, 1, k, cut, down, z > 0)

    def fold(dz, dy, kind):
        ks = (0, 1) if kind == 0 else (2, 3)
        here = exists(dz)
        for k in ks:
            for cut in cuts[k]:
                arrive(dz, dy, k, cut, here)
        pl.when(here)(functools.partial(folded, dz, dy, kind))

    def folded(dz, dy, kind):
        low = (head // 2 + kind) % (head_count // 2) * 2
        place = shard(dz, dy) * head_count + low

        for hd in range(heads_dev):
            cols = slice(hd * HEAD_DIM, (hd + 1) * HEAD_DIM)
            query = q_all[:, :, cols].reshape(tokens, HEAD_DIM)
            old_peak = peak_ref[pl.ds(hd, 1), :]
            new_peak = old_peak
            parts = []
            for n in range(2):
                block = place + n
                gap = query_block - block
                count = jnp.where((gap >= -1) & (gap <= 1), 1, 0)
                for g in range(glob_count):
                    count += jnp.where(glob_ref[g] == block, 1, 0)
                for r in range(rand_count):
                    row = listed[pl.ds(hd * rand_count + r, 1), :]
                    count += jnp.where(row == block, 1, 0)
                count = jnp.where(glob_row > 0, 1, count)
                scores = lax.dot_general(
                    pool[place + n, 0, :, cols], query, (((1,), (1,)), ((), ())),
                    preferred_element_type=jnp.float32,
                ) * (1.0 / math.sqrt(HEAD_DIM))
                top = jnp.max(scores, axis=0, keepdims=True)
                new_peak = jnp.maximum(new_peak, jnp.where(count > 0, top, MASKED))
                parts.append((scores, count))
            fade = jnp.exp(old_peak - new_peak)
            total = total_ref[pl.ds(hd, 1), :] * fade
            acc = acc_ref[hd] * fade
            for n, (scores, count) in enumerate(parts):
                powers = jnp.exp(scores - jnp.where(count > 0, new_peak, -MASKED))
                powers = powers * count.astype(jnp.float32)
                total = total + jnp.sum(powers, axis=0, keepdims=True)
                acc = acc + lax.dot_general(
                    pool[place + n, 1, :, cols], powers.astype(jnp.bfloat16),
                    (((0,), (0,)), ((), ())), preferred_element_type=jnp.float32,
                )
            peak_ref[pl.ds(hd, 1), :] = new_peak
            total_ref[pl.ds(hd, 1), :] = total
            acc_ref[hd] = acc

    own(0)
    for k in others:
        post(q_stage.at[k - 1], q_all.at[head], q_recv_sem.at[head], {"seq": seq, "head": lane(k)})
    own(1)
    own(2)
    hop(0, 1)
    own(3)
    hop(1, 1)
    partner()
    for k in range(1, classes):
        remote(
            q_stage.at[0], q_all.at[lane(k)], send_sem.at[0], q_recv_sem.at[lane(k)], across
        ).wait_recv()
    fold(0, 0, 0)
    hop(2, 1)
    fold(0, 0, 1)
    hop(3, 1)
    fold(0, 1, 0)
    partner_hop(1)
    waiting = [(0, 1, 1)]
    for t in range(1, depth):
        waiting += [(dz, dy, kind) for dy in (0, 1) for kind in (0, 1) for dz in (-t, t)]
        if t + 1 < depth:
            for k in range(classes):
                hop(k, t + 1)
                for item in waiting[:2]:
                    fold(*item)
                waiting = waiting[2:]
            partner_hop(t + 1)
    for item in waiting:
        fold(*item)
    for hd in range(heads_dev):
        done = acc_ref[hd] / total_ref[pl.ds(hd, 1), :]
        out_ref[:, hd * HEAD_DIM : (hd + 1) * HEAD_DIM] = done.T
    for *parts, when in pending:
        pl.when(when)(lambda parts=parts: remote(*parts).wait_send())


def gathered(queries, keys, values, random_blocks, global_blocks):
    seq_count, head_count = lax.axis_size("seq"), lax.axis_size("head")
    rows, width = queries.shape[0], queries.shape[1] // head_count
    heads_dev = width // HEAD_DIM
    tokens = rows * head_count
    rand_count, glob_count = random_blocks.shape[2], global_blocks.shape[0]
    dma = pltpu.SemaphoreType.DMA
    return pl.pallas_call(
        functools.partial(gathered_kernel, seq_count, head_count, rand_count, glob_count),
        out_shape=jax.ShapeDtypeStruct((tokens, width), jnp.float32),
        in_specs=[pl.BlockSpec(memory_space=pltpu.HBM)] * 4
        + [pl.BlockSpec(memory_space=pltpu.SMEM)],
        out_specs=pl.BlockSpec(memory_space=pltpu.VMEM),
        scratch_shapes=[
            pltpu.VMEM((seq_count * head_count, 2, rows, width), jnp.bfloat16),
            pltpu.VMEM(random_blocks.shape, jnp.int32),
            pltpu.VMEM((head_count, rows, width), jnp.bfloat16),
            pltpu.VMEM((head_count - 1, 2, rows, width), jnp.bfloat16),
            pltpu.VMEM((head_count - 1, rows, width), jnp.bfloat16),
            pltpu.VMEM((heads_dev * rand_count, tokens), jnp.int32),
            pltpu.VMEM((heads_dev, tokens), jnp.float32),
            pltpu.VMEM((heads_dev, tokens), jnp.float32),
            pltpu.VMEM((heads_dev, HEAD_DIM, tokens), jnp.float32),
            dma((3 * head_count + 1,)),
            dma((10 * seq_count + 24,)),
            dma((seq_count * head_count, 2)),
            dma((head_count,)),
        ],
        compiler_params=pltpu.CompilerParams(
            collective_id=0, has_side_effects=True
        ),
    )(queries, keys, values, random_blocks, global_blocks)


def shards(queries, keys, values, random_blocks, global_blocks):
    seq_count, head_count = lax.axis_size("seq"), lax.axis_size("head")
    pool_bytes = 4 * seq_count * queries.size
    fits = pool_bytes <= GATHER_LIMIT and queries.shape[0] == BLK
    if fits and head_count == 4 and seq_count % 2 == 0 and seq_count >= 6:
        return gathered(queries, keys, values, random_blocks, global_blocks)
    return exchanged(queries, keys, values, random_blocks, global_blocks)


def solution(mesh):
    in_specs = (
        P(("seq", "head"), None),
        P(("seq", "head"), None),
        P(("seq", "head"), None),
        P("seq", "head", None),
        P(),
    )
    out_specs = P("seq", "head")
    return jax.shard_map(shards, mesh=mesh, in_specs=in_specs, out_specs=out_specs, check_vma=False)
```

profile of v0, /device:TPU:0, one launch (start us, length us, event | category | flops | bytes accessed | tf_op | source)
XLA Modules:
  0.0 53.9 jit_solution(495309970804187614)
XLA Ops:
  0.0 1.4 %copy.6.rand_ref = s32[4,4,3]{2,1,0:T(4,128)} copy(s32[4,4,3]{1,0,2:T(4,128)} %param.8) | data formatting | bytes 384 | tf_op args[3]
  1.4 50.6 %shard_map.55 = f32[256,512]{1,0:T(8,128)} custom-call(bf16[64,2048]{1,0:T(8,128)(2,1)} %q_hbm.1, bf16[64,2048]{1,0:T(8,128)(2,1)} %k_hbm.1, bf16[64,2048]{1,0:T(8,128)(2,1)} %v_hbm.1, s32[4,4,3]{2,1,0:T(4,128)} %copy.6.rand_ref, s32[2]{0:T(128)} %glob_ref.1), custom_call_target="tpu_custom_call" | custom-call | tf_op jit(solution)/shard_map/pallas_call | solution.py:454
  52.0 1.9 %copy.8 = f32[256,512]{1,0:T(8,128)} copy(f32[256,512]{1,0:T(8,128)} %shard_map.55) | data formatting | bytes 1048576
where the time goes:
time: 54.2 us; the launch traced here: 53.9 us
  Pallas kernels  50.6 us (93%)
  local copies, waits for them, and re-layouts  3.25 us (6%)
    pallas_call x1, Pallas kernels, gathered(): pl.pallas_call(functools.partial(gathered_kernel, seq_count, head_count,...  50.6 us
    unnamed x2, local copies, waits for them, and re-layouts  3.25 us

commit v1 on v0

v1 whole, which is shorter than its diff:
```python
import functools
import math

import jax
import jax.numpy as jnp
from jax import lax
from jax.experimental import pallas as pl
from jax.experimental.pallas import tpu as pltpu
from jax.sharding import PartitionSpec as P

HEAD_DIM = 128
BLK = 64


MASKED = -1e30


def extended(block, sides, width):
    for axis, dim in sides:
        count = lax.axis_size(axis)
        forward = [(i, i + 1) for i in range(count - 1)]
        backward = [(target, source) for source, target in forward]
        low = lax.ppermute(
            lax.slice_in_dim(block, block.shape[dim] - width, None, axis=dim), axis, forward
        )
        high = lax.ppermute(lax.slice_in_dim(block, 0, width, axis=dim), axis, backward)
        block = jnp.concatenate([low, block, high], axis=dim)
    return block


def combined_all(value, axis, join):
    pieces = jax.tree.map(lambda part: lax.all_gather(part, axis), value)
    head = jax.tree.map(lambda part: part[0], pieces)
    tail = jax.tree.map(lambda part: part[1:], pieces)
    so_far, _ = lax.scan(lambda so_far, slab: (join(so_far, slab), None), head, tail)
    return so_far


def merge_parts(former, latter):
    peaks = jnp.maximum(former[0], latter[0])
    former_fade = jnp.exp(former[0] - peaks)
    latter_fade = jnp.exp(latter[0] - peaks)
    return (
        peaks,
        former[1] * former_fade + latter[1] * latter_fade,
        former[2] * former_fade[..., None] + latter[2] * latter_fade[..., None],
    )


def soft_parts(scores):
    peaks = jnp.max(scores, axis=(-2, -1))
    powers = jnp.exp(scores - peaks[..., None, None])
    return (peaks, jnp.sum(powers, axis=(-2, -1)), powers.astype(jnp.bfloat16))


def make_requests(rand_lists, seq_count, capacity):
    blk_dev, heads_dev, rand_count = rand_lists.shape
    flat_list = rand_lists.reshape(-1)
    owners = flat_list // blk_dev
    head_ids = jnp.broadcast_to(
        jnp.arange(heads_dev, dtype=jnp.int32)[None, :, None], rand_lists.shape
    ).reshape(-1)
    item_ids = flat_list % blk_dev * heads_dev + head_ids
    position = jnp.arange(flat_list.shape[0], dtype=jnp.int32)
    earlier = (owners[:, None] == owners[None, :]) & (position[None, :] < position[:, None])
    slot_ids = owners * capacity + jnp.sum(earlier.astype(jnp.int32), axis=1)
    requests = jnp.zeros((seq_count * capacity,), jnp.int32).at[slot_ids].set(item_ids)
    sources = jnp.zeros((seq_count * capacity,), jnp.int32).at[slot_ids].set(position)
    return (requests.reshape(seq_count, capacity), slot_ids, sources)


def exchanged(queries, keys, values, random_blocks, global_blocks):
    seq_count = lax.axis_size("seq")
    seq_index = lax.axis_index("seq")
    query_rows, key_rows, value_rows = (
        lax.all_to_all(queries, "head", split_axis=1, concat_axis=0, tiled=True),
        lax.all_to_all(keys, "head", split_axis=1, concat_axis=0, tiled=True),
        lax.all_to_all(values, "head", split_axis=1, concat_axis=0, tiled=True),
    )
    tokens = query_rows.shape[0]
    blk_dev = tokens // BLK
    heads_dev = query_rows.shape[1] // HEAD_DIM
    rand_count = random_blocks.shape[2]
    glob_count = global_blocks.shape[0]
    total_blocks = blk_dev * seq_count
    first_block = seq_index * blk_dev
    capacity = (blk_dev * heads_dev * rand_count * 3 // 2 + seq_count - 1) // seq_count
    score_scale = 1.0 / math.sqrt(HEAD_DIM)
    shape_four = (blk_dev, BLK, heads_dev, HEAD_DIM)
    query_four = query_rows.reshape(shape_four)
    key_four = key_rows.reshape(shape_four)
    value_four = value_rows.reshape(shape_four)
    paired = jnp.stack([key_rows, value_rows])
    padded = extended(paired, (("seq", 1),), BLK)
    padded = padded.reshape(2, blk_dev + 2, BLK, heads_dev, HEAD_DIM)
    window = jnp.stack([padded[:, offset : offset + blk_dev] for offset in range(3)], axis=2)
    near_ids = (
        first_block
        + jnp.arange(blk_dev, dtype=jnp.int32)[:, None]
        + jnp.arange(-1, 2, dtype=jnp.int32)[None, :]
    )
    inside = (near_ids >= 0) & (near_ids < total_blocks)
    stacked = jnp.stack([query_rows, key_rows, value_rows]).reshape(
        3, blk_dev, BLK, heads_dev * HEAD_DIM
    )
    owned_mask = global_blocks // blk_dev == seq_index
    local_ids = jnp.where(owned_mask, global_blocks - first_block, 0)
    picked = (
        jnp.take(stacked, local_ids, axis=1).astype(jnp.float32)
        * owned_mask.astype(jnp.float32)[None, :, None, None]
    )
    glob_rows = lax.psum(picked, "seq").astype(jnp.bfloat16)
    glob_rows = glob_rows.reshape(3, glob_count, BLK, heads_dev, HEAD_DIM)
    requests, slot_ids, sources = make_requests(random_blocks, seq_count, capacity)
    incoming = lax.all_to_all(requests, "seq", split_axis=0, concat_axis=0, tiled=True)

    def by_block(row_data):
        return (
            row_data.reshape(shape_four)
            .transpose(0, 2, 1, 3)
            .reshape(blk_dev * heads_dev, BLK, HEAD_DIM)
        )

    pair_blocks = jnp.stack([by_block(key_rows), by_block(value_rows)], axis=1)
    served = pair_blocks[incoming]
    key_win, value_win = (window[0], window[1])
    win_scores = (
        jnp.einsum("jqhd,jwkhd->jhqwk", query_four, key_win, preferred_element_type=jnp.float32)
        * score_scale
    )
    win_scores = jnp.where(inside[:, None, None, :, None], win_scores, MASKED)
    glob_scores = (
        jnp.einsum("jqhd,gkhd->jhqgk", query_four, glob_rows[1], preferred_element_type=jnp.float32)
        * score_scale
    )
    split_at = 3 + glob_count
    arrived_pairs = lax.all_to_all(served, "seq", split_axis=0, concat_axis=0, tiled=True)
    tail = arrived_pairs.shape[2:]
    rand_pairs = arrived_pairs.reshape((seq_count * capacity,) + tail)[slot_ids].reshape(
        (blk_dev, heads_dev, rand_count) + tail
    )
    rand_scores = (
        jnp.einsum(
            "jqhd,jhrkd->jhqrk",
            query_four,
            rand_pairs[:, :, :, 0],
            preferred_element_type=jnp.float32,
        )
        * score_scale
    )
    peaks, totals, weights = soft_parts(
        jnp.concatenate([win_scores, glob_scores, rand_scores], axis=3)
    )
    sums_all = jnp.einsum(
        "jhqwk,jwkhd->jhqd", weights[:, :, :, 0:3], value_win, preferred_element_type=jnp.float32
    )
    sums_all = sums_all + jnp.einsum(
        "jhqgk,gkhd->jhqd",
        weights[:, :, :, 3:split_at],
        glob_rows[2],
        preferred_element_type=jnp.float32,
    )
    sums_all = sums_all + jnp.einsum(
        "jhqrk,jhrkd->jhqd",
        weights[:, :, :, split_at:],
        rand_pairs[:, :, :, 1],
        preferred_element_type=jnp.float32,
    )
    running = (peaks, totals, sums_all)
    sparse_out = (running[2] / running[1][..., None]).transpose(0, 2, 1, 3)
    full_scores = (
        jnp.einsum("gqhd,jkhd->hgqjk", glob_rows[0], key_four, preferred_element_type=jnp.float32)
        * score_scale
    )
    full_peaks, full_totals, full_weights = soft_parts(full_scores)
    full_sum = jnp.einsum(
        "hgqjk,jkhd->hgqd", full_weights, value_four, preferred_element_type=jnp.float32
    )
    merged = combined_all((full_peaks, full_totals, full_sum), "seq", merge_parts)
    glob_out = (merged[2] / merged[1][..., None]).transpose(1, 2, 0, 3)
    block_ids = first_block + jnp.arange(blk_dev, dtype=jnp.int32)
    result = sparse_out
    for glob_id in range(glob_count):
        matches = (block_ids == global_blocks[glob_id])[:, None, None, None]
        result = jnp.where(matches, glob_out[glob_id][None], result)
    return result.reshape(tokens, heads_dev * HEAD_DIM)


POOL_LIMIT = 16 * 2**20


def headed_kernel(
    seq_count, head_count, rand_count, glob_count,
    q_hbm, k_hbm, v_hbm, rand_hbm, glob_ref, out_hbm,
    k_pool, v_pool, q_pool, rand_vmem, rand_smem, p_buf, tot_buf, full_p, full_tot, full_out,
    o_buf, local_sem, send_sem, k_sem, v_sem, q_sem, o_sem, rand_sem,
):
    seq = lax.axis_index("seq")
    head = lax.axis_index("head")
    depth = seq_count // 2
    lanes = head_count // 2
    z, y = seq // 2, seq % 2
    x, core = head // 2, head % 2
    heads_dev = seq_count // 2
    span = seq_count * lanes
    blocks = 2 * span
    mine = 2 * (seq * lanes + x) + core
    group = 2 * x + seq // heads_dev
    column = seq % heads_dev
    partner = {"seq": seq, "head": 2 * x + 1 - core}
    scale = 1.0 / math.sqrt(HEAD_DIM)

    def seq_at(dz, dy):
        return (z + dz) % depth * 2 + (y + dy) % 2

    offsets = [
        (dz, dy, dx)
        for dz in list(range(1, depth)) + [0]
        for dy in range(2)
        for dx in range(lanes)
        if (dz, dy, dx) != (0, 0, 0)
    ]

    pending = []

    def remote(source, dest, sender, receiver, device):
        return pltpu.make_async_remote_copy(
            src_ref=source, dst_ref=dest, send_sem=sender, recv_sem=receiver,
            device_id=device, device_id_type=pl.DeviceIdType.MESH,
        )

    def post(source, dest, receiver, device):
        copy = remote(source, dest, send_sem.at[len(pending)], receiver, device)
        pending.append((copy, None))
        copy.start()

    def post_or_keep(source, dest, receiver, device, here):
        sender = send_sem.at[len(pending)]
        copy = remote(source, dest, sender, receiver, device)
        kept = pltpu.make_async_copy(source, dest, receiver)
        pl.when(here)(lambda: kept.start())
        pl.when(jnp.logical_not(here))(lambda: copy.start())
        pending.append((copy, jnp.logical_not(here)))

    def arrive(piece, receiver):
        remote(piece, piece, send_sem.at[0], receiver, partner).wait_recv()

    barrier = pltpu.get_barrier_semaphore()
    greeted = 0
    for ds in range(seq_count):
        for dh in range(head_count):
            if ds or dh:
                friend = {"seq": (seq + ds) % seq_count, "head": (head + dh) % head_count}
                pl.semaphore_signal(
                    barrier, inc=1, device_id=friend, device_id_type=pl.DeviceIdType.MESH
                )
                greeted += 1

    own_cols = pl.ds(pl.multiple_of((x * seq_count + seq) * HEAD_DIM, HEAD_DIM), HEAD_DIM)
    slot = mine // 2
    own = [
        pltpu.make_async_copy(k_hbm.at[:, own_cols], k_pool.at[mine + 1], local_sem.at[0]),
        pltpu.make_async_copy(q_hbm.at[:, own_cols], q_pool.at[slot], local_sem.at[1]),
        pltpu.make_async_copy(v_hbm.at[:, own_cols], v_pool.at[mine + 1], local_sem.at[2]),
    ]
    for copy in own:
        copy.start()
    blank = jnp.zeros((BLK, HEAD_DIM), jnp.bfloat16)
    for pool in (k_pool, v_pool):
        pool[0] = blank
        pool[blocks + 1] = blank
    pl.semaphore_wait(barrier, greeted)

    def scatter(source, dest, receiver):
        for dz, dy, dx in offsets:
            there, lane = seq_at(dz, dy), (x + dx) % lanes
            cols = pl.ds(pl.multiple_of((lane * seq_count + there) * HEAD_DIM, HEAD_DIM), HEAD_DIM)
            post(source.at[:, cols], dest, receiver, {"seq": there, "head": 2 * lane + core})

    for there in range(heads_dev):
        owner = head % 2 * heads_dev + there
        for other in range(2):
            post_or_keep(
                rand_hbm, rand_vmem.at[seq], rand_sem.at[seq], {"seq": owner, "head": 2 * x + other},
                (owner == seq) & (core == other),
            )
    scatter(k_hbm, k_pool.at[mine + 1], k_sem.at[mine])
    scatter(q_hbm, q_pool.at[slot], q_sem.at[slot])
    scatter(v_hbm, v_pool.at[mine + 1], v_sem.at[mine])

    def source_slot(dz, dy, dx):
        return seq_at(-dz, -dy) * lanes + (x - dx) % lanes

    def pass_on(pool, own_copy, sems):
        own_copy.wait()
        post(pool.at[mine + 1], pool.at[mine + 1], sems.at[mine], partner)
        for offset in offsets:
            block = 2 * source_slot(*offset) + core
            arrive(pool.at[block + 1], sems.at[block])
            post(pool.at[block + 1], pool.at[block + 1], sems.at[block], partner)

    def collect(pool, sems):
        for n in range(span):
            block = 2 * n + 1 - core
            arrive(pool.at[block + 1], sems.at[block])

    pass_on(k_pool, own[0], k_sem)
    for s in range(seq_count):
        arrive(rand_vmem.at[s], rand_sem.at[s])
    names = pltpu.make_async_copy(rand_vmem, rand_smem, local_sem.at[3])
    names.start()
    own[1].wait()
    for offset in offsets:
        n = source_slot(*offset)
        arrive(q_pool.at[n], q_sem.at[n])
    collect(k_pool, k_sem)
    names.wait()

    def key_set(pool, n):
        s, lane = n // lanes, n % lanes
        block = 2 * n + core
        parts = [pool[pl.ds(block, 3)].reshape(3 * BLK, HEAD_DIM)]
        parts += [pool[glob_ref[g] + 1] for g in range(glob_count)]
        parts += [
            pool[rand_smem[s, r, 2 * lane + core, column] + 1] for r in range(rand_count)
        ]
        return jnp.concatenate(parts, axis=0)

    def soften(scores):
        peaks = jnp.max(scores, axis=1, keepdims=True)
        powers = jnp.exp(scores - peaks)
        return powers.astype(jnp.bfloat16), jnp.sum(powers, axis=1, keepdims=True)

    def scored(query, keys):
        return lax.dot_general(
            query, keys, (((1,), (1,)), ((), ())), preferred_element_type=jnp.float32
        ) * scale

    for n in range(span):
        scores = scored(q_pool[n], key_set(k_pool, n))
        place = lax.broadcasted_iota(jnp.int32, scores.shape, 1) // BLK
        if n == 0:
            scores = jnp.where((place == 0) & (core == 0), MASKED, scores)
        if n == span - 1:
            scores = jnp.where((place == 2) & (core == 1), MASKED, scores)
        powers, totals = soften(scores)
        p_buf[n] = powers
        tot_buf[n] = jnp.broadcast_to(totals, (BLK, HEAD_DIM))
    every = pl.ds(1, blocks)
    for g in range(glob_count):
        powers, totals = soften(
            scored(q_pool[glob_ref[g] // 2], k_pool[every].reshape(blocks * BLK, HEAD_DIM))
        )
        full_p[g] = powers
        full_tot[g] = jnp.broadcast_to(totals, (BLK, HEAD_DIM))

    pass_on(v_pool, own[2], v_sem)
    collect(v_pool, v_sem)

    def summed(powers, values):
        return lax.dot_general(
            powers, values, (((1,), (0,)), ((), ())), preferred_element_type=jnp.float32
        )

    for g in range(glob_count):
        full_out[g] = (
            summed(full_p[g], v_pool[every].reshape(blocks * BLK, HEAD_DIM)) / full_tot[g]
        )

    def send(n):
        s, lane = n // lanes, n % lanes
        dest = out_hbm.at[
            pl.ds(pl.multiple_of((2 * lane + core) * BLK, BLK), BLK),
            pl.ds(pl.multiple_of(column * HEAD_DIM, HEAD_DIM), HEAD_DIM),
        ]
        post_or_keep(
            o_buf.at[n], dest, o_sem.at[column, 2 * lane + core], {"seq": s, "head": group},
            (seq == s) & (head == group),
        )

    for n in range(span):
        result = summed(p_buf[n], key_set(v_pool, n)) / tot_buf[n]
        for g in range(glob_count):
            result = jnp.where(glob_ref[g] == 2 * n + core, full_out[g], result)
        o_buf[n] = result.astype(jnp.bfloat16)
        if n > 0:
            send(n - 1)
    send(span - 1)
    for col in range(heads_dev):
        for row in range(head_count):
            piece = out_hbm.at[
                row * BLK : (row + 1) * BLK, col * HEAD_DIM : (col + 1) * HEAD_DIM
            ]
            arrive(piece, o_sem.at[col, row])
    for copy, when in pending:
        if when is None:
            copy.wait_send()
        else:
            pl.when(when)(lambda copy=copy: copy.wait_send())


def headed(queries, keys, values, random_blocks, global_blocks):
    seq_count, head_count = lax.axis_size("seq"), lax.axis_size("head")
    heads_dev = queries.shape[1] // HEAD_DIM // head_count
    rand_count, glob_count = random_blocks.shape[2], global_blocks.shape[0]
    names = random_blocks.transpose(2, 0, 1)
    span = seq_count * head_count // 2
    blocks = 2 * span
    width = (3 + glob_count + rand_count) * BLK
    dma = pltpu.SemaphoreType.DMA
    tile = (BLK, HEAD_DIM)
    result = pl.pallas_call(
        functools.partial(headed_kernel, seq_count, head_count, rand_count, glob_count),
        out_shape=jax.ShapeDtypeStruct((head_count * BLK, heads_dev * HEAD_DIM), jnp.bfloat16),
        in_specs=[pl.BlockSpec(memory_space=pltpu.HBM)] * 4
        + [pl.BlockSpec(memory_space=pltpu.SMEM)],
        out_specs=pl.BlockSpec(memory_space=pltpu.HBM),
        scratch_shapes=[
            pltpu.VMEM((blocks + 2,) + tile, jnp.bfloat16),
            pltpu.VMEM((blocks + 2,) + tile, jnp.bfloat16),
            pltpu.VMEM((span,) + tile, jnp.bfloat16),
            pltpu.VMEM((seq_count,) + names.shape, jnp.int32),
            pltpu.SMEM((seq_count,) + names.shape, jnp.int32),
            pltpu.VMEM((span, BLK, width), jnp.bfloat16),
            pltpu.VMEM((span,) + tile, jnp.float32),
            pltpu.VMEM((glob_count, BLK, blocks * BLK), jnp.bfloat16),
            pltpu.VMEM((glob_count,) + tile, jnp.float32),
            pltpu.VMEM((glob_count,) + tile, jnp.float32),
            pltpu.VMEM((span,) + tile, jnp.bfloat16),
            dma((4,)),
            dma((6 * span + 2 * heads_dev,)),
            dma((blocks,)),
            dma((blocks,)),
            dma((span,)),
            dma((heads_dev, head_count)),
            dma((seq_count,)),
        ],
        compiler_params=pltpu.CompilerParams(
            collective_id=0, has_side_effects=True
        ),
    )(queries, keys, values, names, global_blocks)
    return result.astype(jnp.float32)


def shards(queries, keys, values, random_blocks, global_blocks):
    seq_count, head_count = lax.axis_size("seq"), lax.axis_size("head")
    rows, width = queries.shape
    span = seq_count * head_count // 2
    fits = 6 * rows * width * span // head_count <= POOL_LIMIT
    even = seq_count % 2 == 0 and head_count % 2 == 0
    if fits and even and rows == BLK and width == span * HEAD_DIM:
        return headed(queries, keys, values, random_blocks, global_blocks)
    return exchanged(queries, keys, values, random_blocks, global_blocks)


def solution(mesh):
    in_specs = (
        P(("seq", "head"), None),
        P(("seq", "head"), None),
        P(("seq", "head"), None),
        P("seq", "head", None),
        P(),
    )
    out_specs = P("seq", "head")
    return jax.shard_map(shards, mesh=mesh, in_specs=in_specs, out_specs=out_specs, check_vma=False)
```

time: 54.2 us -> 38.8 us (0.72)
  the two profiles are of different devices: /device:TPU:0 before, /device:TPU:24 now
where the time goes in v1:
time: 38.8 us; the launch traced here: 38.7 us
  Pallas kernels  36.9 us (95%)
  other arithmetic  1.8 us (5%)
    pallas_call x1, Pallas kernels, headed(): pl.pallas_call(functools.partial(headed_kernel, seq_count, head_count, ra...  36.9 us
    convert_element_type x1, other arithmetic, headed(): return result.astype(jnp.float32)  1.8 us

profile of v1, /device:TPU:24, one launch (start us, length us, event | category | flops | bytes accessed | tf_op | source)
XLA Modules:
  0.0 38.7 jit_solution(6397452158553589094)
XLA Ops:
  0.0 36.9 %shard_map.55 = bf16[256,512]{1,0:T(8,128)(2,1)} custom-call(bf16[64,2048]{1,0:T(8,128)(2,1)} %q_hbm.1, bf16[64,2048]{1,0:T(8,128)(2,1)} %k_hbm.1, bf16[64,2048]{1,0:T(8,128)(2,1)} %v_hbm.1, s32[3,4,4]{2,1,0:T(4,128)} %bitcast.1, s32[2]{0:T(128)} %glob_ref.1), custom_call_target="tpu_custom_call" | custom-call | tf_op jit(solution)/shard_map/pallas_call | solution.py:412
  36.9 1.8 %convert_element_type.3 = f32[256,512]{1,0:T(8,128)} convert(bf16[256,512]{1,0:T(8,128)(2,1)} %shard_map.55) | non-fusion elementwise | flops 131072 | bytes 786432 | tf_op jit(solution)/shard_map/convert_element_type | solution.py:442

commit v2 on v1

--- a/solution.py
+++ b/solution.py
@@ -190,10 +190,11 @@
 
 
 def headed_kernel(
-    seq_count, head_count, rand_count, glob_count,
-    q_hbm, k_hbm, v_hbm, rand_hbm, glob_ref, out_hbm,
-    k_pool, v_pool, q_pool, rand_vmem, rand_smem, p_buf, tot_buf, full_p, full_tot, full_out,
-    o_buf, local_sem, send_sem, k_sem, v_sem, q_sem, o_sem, rand_sem,
+    seq_count, head_count, rand_count,
+    q_hbm, k_hbm, v_hbm, rand_hbm, glob_ref, out_ref,
+    k_pool, v_pool, q_early, q_late, rand_own, rand_tile, rand_vmem, rand_smem, p_buf, tot_buf, full_p, full_tot,
+    full_out, o_buf, local_sem, send_sem, pass_sem, rand_send, o_send,
+    k_sem, v_sem, q_sem, o_sem, rand_sem,
 ):
     seq = lax.axis_index("seq")
     head = lax.axis_index("head")
@@ -204,49 +205,34 @@
     heads_dev = seq_count // 2
     span = seq_count * lanes
     blocks = 2 * span
-    mine = 2 * (seq * lanes + x) + core
+    late_lanes = lanes // 2
+    early_lanes = lanes - late_lanes
+    slot = seq * lanes + x
+    mine = 2 * slot + core
     group = 2 * x + seq // heads_dev
     column = seq % heads_dev
     partner = {"seq": seq, "head": 2 * x + 1 - core}
+    last = blocks - 1
+    other = jnp.clip(glob_ref[0] + glob_ref[1] - last, 0, last)
     scale = 1.0 / math.sqrt(HEAD_DIM)
 
-    def seq_at(dz, dy):
-        return (z + dz) % depth * 2 + (y + dy) % 2
-
-    offsets = [
-        (dz, dy, dx)
-        for dz in list(range(1, depth)) + [0]
-        for dy in range(2)
-        for dx in range(lanes)
-        if (dz, dy, dx) != (0, 0, 0)
-    ]
-
-    pending = []
-
-    def remote(source, dest, sender, receiver, device):
+    def device(there, lane):
+        return {"seq": there, "head": 2 * lane + core}
+
+    def remote(source, dest, sender, receiver, target):
         return pltpu.make_async_remote_copy(
             src_ref=source, dst_ref=dest, send_sem=sender, recv_sem=receiver,
-            device_id=device, device_id_type=pl.DeviceIdType.MESH,
-        )
-
-    def post(source, dest, receiver, device):
-        copy = remote(source, dest, send_sem.at[len(pending)], receiver, device)
-        pending.append((copy, None))
-        copy.start()
-
-    def post_or_keep(source, dest, receiver, device, here):
-        sender = send_sem.at[len(pending)]
-        copy = remote(source, dest, sender, receiver, device)
-        kept = pltpu.make_async_copy(source, dest, receiver)
-        pl.when(here)(lambda: kept.start())
-        pl.when(jnp.logical_not(here))(lambda: copy.start())
-        pending.append((copy, jnp.logical_not(here)))
+            device_id=target, device_id_type=pl.DeviceIdType.MESH,
+        )
 
     def arrive(piece, receiver):
-        remote(piece, piece, send_sem.at[0], receiver, partner).wait_recv()
+        remote(piece, piece, local_sem.at[0], receiver, partner).wait_recv()
+
+    def leave(piece, sender):
+        remote(piece, piece, sender, local_sem.at[0], partner).wait_send()
 
     barrier = pltpu.get_barrier_semaphore()
-    greeted = 0
+    friends = 0
     for ds in range(seq_count):
         for dh in range(head_count):
             if ds or dh:
@@ -254,186 +240,285 @@
                 pl.semaphore_signal(
                     barrier, inc=1, device_id=friend, device_id_type=pl.DeviceIdType.MESH
                 )
-                greeted += 1
-
-    own_cols = pl.ds(pl.multiple_of((x * seq_count + seq) * HEAD_DIM, HEAD_DIM), HEAD_DIM)
-    slot = mine // 2
-    own = [
-        pltpu.make_async_copy(k_hbm.at[:, own_cols], k_pool.at[mine + 1], local_sem.at[0]),
-        pltpu.make_async_copy(q_hbm.at[:, own_cols], q_pool.at[slot], local_sem.at[1]),
-        pltpu.make_async_copy(v_hbm.at[:, own_cols], v_pool.at[mine + 1], local_sem.at[2]),
-    ]
-    for copy in own:
-        copy.start()
+                friends += 1
+
+    def columns(there, lane):
+        return pl.ds(pl.multiple_of((lane * seq_count + there) * HEAD_DIM, HEAD_DIM), HEAD_DIM)
+
+    here = columns(seq, x)
+    pltpu.make_async_copy(k_hbm.at[:, here], k_pool.at[mine + 1], k_sem.at[mine]).start()
+    pltpu.make_async_copy(v_hbm.at[:, here], v_pool.at[mine + 1], v_sem.at[mine]).start()
+
+    pltpu.make_async_copy(
+        q_hbm.at[:, here], q_early.at[seq * early_lanes], q_sem.at[slot]
+    ).start()
     blank = jnp.zeros((BLK, HEAD_DIM), jnp.bfloat16)
     for pool in (k_pool, v_pool):
         pool[0] = blank
         pool[blocks + 1] = blank
-    pl.semaphore_wait(barrier, greeted)
-
-    def scatter(source, dest, receiver):
-        for dz, dy, dx in offsets:
-            there, lane = seq_at(dz, dy), (x + dx) % lanes
-            cols = pl.ds(pl.multiple_of((lane * seq_count + there) * HEAD_DIM, HEAD_DIM), HEAD_DIM)
-            post(source.at[:, cols], dest, receiver, {"seq": there, "head": 2 * lane + core})
-
+
+    own_names = pltpu.make_async_copy(
+        rand_hbm, rand_own.at[pl.ds(0, rand_count)], local_sem.at[1]
+    )
+    own_names.start()
+    rand_tile[...] = jnp.zeros_like(rand_tile)
+    own_names.wait()
+    for r in range(rand_count):
+        rand_tile[:head_count, r * heads_dev : (r + 1) * heads_dev] = rand_own[r]
+    pl.semaphore_wait(barrier, friends)
+
+    steps = list(range(1, depth)) + [0]
+
+    def push(kind, source, dest, receiver, lane_steps):
+        for step in steps:
+            for dy in range(2):
+                for dx in lane_steps:
+                    if step or dy or dx:
+                        there, lane = 2 * ((z + step) % depth) + (y + dy) % 2, (x + dx) % lanes
+                        sender = send_sem.at[kind, (step * 2 + dy) * lanes + dx]
+                        remote(
+                            source.at[:, columns(there, lane)], dest(dx), sender, receiver,
+                            device(there, lane),
+                        ).start()
+
+    def post_or_keep(source, dest, sender, receiver, target, at_home):
+        copy = remote(source, dest, sender, receiver, target)
+        kept = pltpu.make_async_copy(source, dest, receiver)
+        pl.when(at_home)(lambda: kept.start())
+        pl.when(jnp.logical_not(at_home))(lambda: copy.start())
+
+    lead = seq // heads_dev
+
+    def owner_of(there):
+        return head % 2 * heads_dev + there
+
+    everyone = range(lanes)
+    push(0, k_hbm, lambda dx: k_pool.at[mine + 1], k_sem.at[mine], everyone)
     for there in range(heads_dev):
-        owner = head % 2 * heads_dev + there
-        for other in range(2):
-            post_or_keep(
-                rand_hbm, rand_vmem.at[seq], rand_sem.at[seq], {"seq": owner, "head": 2 * x + other},
-                (owner == seq) & (core == other),
-            )
-    scatter(k_hbm, k_pool.at[mine + 1], k_sem.at[mine])
-    scatter(q_hbm, q_pool.at[slot], q_sem.at[slot])
-    scatter(v_hbm, v_pool.at[mine + 1], v_sem.at[mine])
-
-    def source_slot(dz, dy, dx):
-        return seq_at(-dz, -dy) * lanes + (x - dx) % lanes
-
-    def pass_on(pool, own_copy, sems):
-        own_copy.wait()
-        post(pool.at[mine + 1], pool.at[mine + 1], sems.at[mine], partner)
-        for offset in offsets:
-            block = 2 * source_slot(*offset) + core
-            arrive(pool.at[block + 1], sems.at[block])
-            post(pool.at[block + 1], pool.at[block + 1], sems.at[block], partner)
+        post_or_keep(
+            rand_tile, rand_vmem.at[seq], rand_send.at[there], rand_sem.at[seq],
+            {"seq": owner_of(there), "head": head}, owner_of(there) == seq,
+        )
+    push(
+        2, q_hbm, lambda dx: q_early.at[seq * early_lanes + dx], q_sem.at[slot], range(early_lanes)
+    )
+    push(1, v_hbm, lambda dx: v_pool.at[mine + 1], v_sem.at[mine], everyone)
+    push(
+        2, q_hbm, lambda dx: q_late.at[seq * late_lanes + dx - early_lanes], q_sem.at[slot],
+        range(early_lanes, lanes),
+    )
+
+    def slots(lane_steps):
+        return [(s, dx, (x - dx) % lanes) for s in range(seq_count) for dx in lane_steps]
+
+    early = slots(range(early_lanes))
+    late = slots(range(early_lanes, lanes))
+
+    def pass_on(kind, pool, sems):
+        arrivals = [
+            (2 * ((z - step) % depth) + (y + dy) % 2, (x - dx) % lanes)
+            for step in steps[::-1]
+            for dy in range(2)
+            for dx in everyone
+        ]
+        for place, (s, lane) in enumerate(arrivals):
+            block = 2 * (s * lanes + lane) + core
+            piece = pool.at[block + 1]
+            arrive(piece, sems.at[block])
+            remote(piece, piece, pass_sem.at[kind, place], sems.at[block], partner).start()
 
     def collect(pool, sems):
         for n in range(span):
             block = 2 * n + 1 - core
             arrive(pool.at[block + 1], sems.at[block])
 
-    pass_on(k_pool, own[0], k_sem)
-    for s in range(seq_count):
-        arrive(rand_vmem.at[s], rand_sem.at[s])
-    names = pltpu.make_async_copy(rand_vmem, rand_smem, local_sem.at[3])
+    pass_on(0, k_pool, k_sem)
+    shared = remote(rand_vmem, rand_vmem, rand_send.at[heads_dev], rand_sem.at[seq_count], partner)
+
+    def share_names():
+        for s in range(seq_count):
+            arrive(rand_vmem.at[s], rand_sem.at[s])
+        shared.start()
+
+    pl.when(core == lead)(share_names)
+    pl.when(core != lead)(lambda: shared.wait_recv())
+    names = pltpu.make_async_copy(rand_vmem, rand_smem, local_sem.at[1])
     names.start()
-    own[1].wait()
-    for offset in offsets:
-        n = source_slot(*offset)
-        arrive(q_pool.at[n], q_sem.at[n])
+    for s, dx, lane in early:
+        arrive(q_early.at[s * early_lanes + dx], q_sem.at[s * lanes + lane])
     collect(k_pool, k_sem)
     names.wait()
 
-    def key_set(pool, n):
-        s, lane = n // lanes, n % lanes
-        block = 2 * n + core
-        parts = [pool[pl.ds(block, 3)].reshape(3 * BLK, HEAD_DIM)]
-        parts += [pool[glob_ref[g] + 1] for g in range(glob_count)]
+    def key_set(pool, s, lane):
+        parts = [pool[pl.ds(2 * (s * lanes + lane) + core, 3)].reshape(3 * BLK, HEAD_DIM)]
+        parts += [pool[glob_ref[g] + 1] for g in range(2)]
         parts += [
-            pool[rand_smem[s, r, 2 * lane + core, column] + 1] for r in range(rand_count)
+            pool[rand_smem[s, 2 * lane + core, r * heads_dev + column] + 1] for r in range(rand_count)
         ]
         return jnp.concatenate(parts, axis=0)
 
     def soften(scores):
         peaks = jnp.max(scores, axis=1, keepdims=True)
         powers = jnp.exp(scores - peaks)
-        return powers.astype(jnp.bfloat16), jnp.sum(powers, axis=1, keepdims=True)
+        totals = jnp.sum(powers, axis=1, keepdims=True)
+        return powers.astype(jnp.bfloat16), jnp.broadcast_to(totals, (totals.shape[0], HEAD_DIM))
 
     def scored(query, keys):
         return lax.dot_general(
             query, keys, (((1,), (1,)), ((), ())), preferred_element_type=jnp.float32
         ) * scale
 
-    for n in range(span):
-        scores = scored(q_pool[n], key_set(k_pool, n))
-        place = lax.broadcasted_iota(jnp.int32, scores.shape, 1) // BLK
-        if n == 0:
-            scores = jnp.where((place == 0) & (core == 0), MASKED, scores)
-        if n == span - 1:
-            scores = jnp.where((place == 2) & (core == 1), MASKED, scores)
-        powers, totals = soften(scores)
-        p_buf[n] = powers
-        tot_buf[n] = jnp.broadcast_to(totals, (BLK, HEAD_DIM))
-    every = pl.ds(1, blocks)
-    for g in range(glob_count):
-        powers, totals = soften(
-            scored(q_pool[glob_ref[g] // 2], k_pool[every].reshape(blocks * BLK, HEAD_DIM))
-        )
-        full_p[g] = powers
-        full_tot[g] = jnp.broadcast_to(totals, (BLK, HEAD_DIM))
-
-    pass_on(v_pool, own[2], v_sem)
-    collect(v_pool, v_sem)
-
     def summed(powers, values):
         return lax.dot_general(
             powers, values, (((1,), (0,)), ((), ())), preferred_element_type=jnp.float32
         )
 
-    for g in range(glob_count):
-        full_out[g] = (
-            summed(full_p[g], v_pool[every].reshape(blocks * BLK, HEAD_DIM)) / full_tot[g]
-        )
-
-    def send(n):
-        s, lane = n // lanes, n % lanes
-        dest = out_hbm.at[
-            pl.ds(pl.multiple_of((2 * lane + core) * BLK, BLK), BLK),
-            pl.ds(pl.multiple_of(column * HEAD_DIM, HEAD_DIM), HEAD_DIM),
-        ]
+    edge = 4 * BLK
+
+    def sparse_scores(query, s, lane):
+        scores = scored(query, key_set(k_pool, s, lane))
+        near = scores[:, :edge]
+        place = lax.broadcasted_iota(jnp.int32, near.shape, 1) // BLK
+        block = 2 * (s * lanes + lane) + core
+        outside = ((place == 0) & (block == 0)) | ((place == 2) & (block == last))
+        return jnp.concatenate([jnp.where(outside, MASKED, near), scores[:, edge:]], axis=1)
+
+    every = pl.ds(1, blocks)
+
+    def whole(pool):
+        return pool[every].reshape(blocks * BLK, HEAD_DIM)
+
+    for n, (s, dx, lane) in enumerate(early):
+        p_buf[n], tot_buf[n] = soften(
+            sparse_scores(q_early[s * early_lanes + dx], s, lane)
+        )
+    other_seq = other // head_count
+    other_step = (x - other % head_count // 2) % lanes
+    last_step = (x - lanes + 1) % lanes
+
+    def pair(pool, count, first):
+        last_place = (seq_count - 1) * count + jnp.clip(last_step - first, 0, count - 1)
+        other_place = other_seq * count + jnp.clip(other_step - first, 0, count - 1)
+        return jnp.concatenate([pool[last_place], pool[other_place]], axis=0)
+
+    full_p[...], full_tot[...] = soften(scored(pair(q_early, early_lanes, 0), whole(k_pool)))
+
+    pass_on(1, v_pool, v_sem)
+    collect(v_pool, v_sem)
+    full_out[...] = summed(full_p[...], whole(v_pool)) / full_tot[...]
+
+    def send(s, lane):
+        n = s * lanes + lane
+        rows = pl.ds(pl.multiple_of((2 * lane + core) * BLK, BLK), BLK)
+        cols = pl.ds(pl.multiple_of(column * HEAD_DIM, HEAD_DIM), HEAD_DIM)
         post_or_keep(
-            o_buf.at[n], dest, o_sem.at[column, 2 * lane + core], {"seq": s, "head": group},
-            (seq == s) & (head == group),
-        )
-
-    for n in range(span):
-        result = summed(p_buf[n], key_set(v_pool, n)) / tot_buf[n]
-        for g in range(glob_count):
-            result = jnp.where(glob_ref[g] == 2 * n + core, full_out[g], result)
-        o_buf[n] = result.astype(jnp.bfloat16)
-        if n > 0:
-            send(n - 1)
-    send(span - 1)
+            o_buf.at[n], out_ref.at[rows, cols], o_send.at[n], o_sem.at[column, 2 * lane + core],
+            {"seq": s, "head": group}, (seq == s) & (head == group),
+        )
+
+    def finish(result, s, lane):
+        block = 2 * (s * lanes + lane) + core
+        result = jnp.where(last == block, full_out[:BLK], result)
+        result = jnp.where(other == block, full_out[BLK:], result)
+        o_buf[s * lanes + lane] = result.astype(jnp.bfloat16)
+
+    ready = None
+    for n, (s, dx, lane) in enumerate(early):
+        finish(summed(p_buf[n], key_set(v_pool, s, lane)) / tot_buf[n], s, lane)
+        if ready:
+            send(*ready)
+        ready = (s, lane)
+    send(*ready)
+    if late:
+        for s, dx, lane in late:
+            arrive(q_late.at[s * late_lanes + dx - early_lanes], q_sem.at[s * lanes + lane])
+        powers, totals = soften(scored(pair(q_late, late_lanes, early_lanes), whole(k_pool)))
+        full_out[...] = summed(powers, whole(v_pool)) / totals
+        ready = None
+        for s, dx, lane in late:
+            query = q_late[s * late_lanes + dx - early_lanes]
+            powers, totals = soften(sparse_scores(query, s, lane))
+            finish(summed(powers, key_set(v_pool, s, lane)) / totals, s, lane)
+            if ready:
+                send(*ready)
+            ready = (s, lane)
+        send(*ready)
+
+    tile = k_pool.at[0]
+    for kind in range(3):
+        for n in range(1, span):
+            leave(tile, send_sem.at[kind, n])
+    for kind in range(2):
+        for place in range(span):
+            leave(tile, pass_sem.at[kind, place])
+    for there in range(heads_dev):
+        pl.when(owner_of(there) != seq)(
+            lambda there=there: leave(rand_tile, rand_send.at[there])
+        )
+    pl.when(core == lead)(lambda: shared.wait_send())
+    for s, dx, lane in early + late:
+        pl.when((seq != s) | (head != group))(
+            lambda s=s, lane=lane: leave(tile, o_send.at[s * lanes + lane])
+        )
     for col in range(heads_dev):
         for row in range(head_count):
-            piece = out_hbm.at[
+            piece = out_ref.at[
                 row * BLK : (row + 1) * BLK, col * HEAD_DIM : (col + 1) * HEAD_DIM
             ]
             arrive(piece, o_sem.at[col, row])
-    for copy, when in pending:
-        if when is None:
-            copy.wait_send()
-        else:
-            pl.when(when)(lambda copy=copy: copy.wait_send())
 
 
 def headed(queries, keys, values, random_blocks, global_blocks):
     seq_count, head_count = lax.axis_size("seq"), lax.axis_size("head")
     heads_dev = queries.shape[1] // HEAD_DIM // head_count
-    rand_count, glob_count = random_blocks.shape[2], global_blocks.shape[0]
+    rand_count = random_blocks.shape[2]
     names = random_blocks.transpose(2, 0, 1)
-    span = seq_count * head_count // 2
+    lanes = head_count // 2
+    late_lanes = lanes // 2
+    early_count, late_count = seq_count * (lanes - late_lanes), max(seq_count * late_lanes, 1)
+    span = seq_count * lanes
     blocks = 2 * span
-    width = (3 + glob_count + rand_count) * BLK
+    width = (5 + rand_count) * BLK
     dma = pltpu.SemaphoreType.DMA
-    tile = (BLK, HEAD_DIM)
+    tile, name_tile = (BLK, HEAD_DIM), (8, 128)
+
+    def bf16(*shape):
+        return pltpu.VMEM(shape, jnp.bfloat16)
+
+    def f32(*shape):
+        return pltpu.VMEM(shape, jnp.float32)
+
     result = pl.pallas_call(
-        functools.partial(headed_kernel, seq_count, head_count, rand_count, glob_count),
-        out_shape=jax.ShapeDtypeStruct((head_count * BLK, heads_dev * HEAD_DIM), jnp.bfloat16),
+        functools.partial(headed_kernel, seq_count, head_count, rand_count),
+        out_shape=bf16(head_count * BLK, heads_dev * HEAD_DIM),
         in_specs=[pl.BlockSpec(memory_space=pltpu.HBM)] * 4
         + [pl.BlockSpec(memory_space=pltpu.SMEM)],
-        out_specs=pl.BlockSpec(memory_space=pltpu.HBM),
+        out_specs=pl.BlockSpec(memory_space=pl.ANY),
         scratch_shapes=[
-            pltpu.VMEM((blocks + 2,) + tile, jnp.bfloat16),
-            pltpu.VMEM((blocks + 2,) + tile, jnp.bfloat16),
-            pltpu.VMEM((span,) + tile, jnp.bfloat16),
-            pltpu.VMEM((seq_count,) + names.shape, jnp.int32),
-            pltpu.SMEM((seq_count,) + names.shape, jnp.int32),
-            pltpu.VMEM((span, BLK, width), jnp.bfloat16),
-            pltpu.VMEM((span,) + tile, jnp.float32),
-            pltpu.VMEM((glob_count, BLK, blocks * BLK), jnp.bfloat16),
-            pltpu.VMEM((glob_count,) + tile, jnp.float32),
-            pltpu.VMEM((glob_count,) + tile, jnp.float32),
-            pltpu.VMEM((span,) + tile, jnp.bfloat16),
-            dma((4,)),
-            dma((6 * span + 2 * heads_dev,)),
+            bf16(blocks + 2, *tile),
+            bf16(blocks + 2, *tile),
+            bf16(early_count, *tile),
+            bf16(late_count, *tile),
+            pltpu.VMEM((rand_count + 1,) + names.shape[1:], jnp.int32),
+            pltpu.VMEM(name_tile, jnp.int32),
+            pltpu.VMEM((seq_count,) + name_tile, jnp.int32),
+            pltpu.SMEM((seq_count,) + name_tile, jnp.int32),
+            bf16(early_count, BLK, width),
+            f32(early_count, *tile),
+            bf16(2 * BLK, blocks * BLK),
+            f32(2 * BLK, HEAD_DIM),
+            f32(2 * BLK, HEAD_DIM),
+            bf16(span, *tile),
+            dma((2,)),
+            dma((3, span)),
+            dma((2, span)),
+            dma((heads_dev + 1,)),
+            dma((span,)),
             dma((blocks,)),
             dma((blocks,)),
             dma((span,)),
             dma((heads_dev, head_count)),
-            dma((seq_count,)),
+            dma((seq_count + 1,)),
         ],
         compiler_params=pltpu.CompilerParams(
             collective_id=0, has_side_effects=True
@@ -447,7 +532,7 @@
     rows, width = queries.shape
     span = seq_count * head_count // 2
     fits = 6 * rows * width * span // head_count <= POOL_LIMIT
-    even = seq_count % 2 == 0 and head_count % 2 == 0
+    even = seq_count % 2 == 0 and head_count % 2 == 0 and global_blocks.shape[0] == 2
     if fits and even and rows == BLK and width == span * HEAD_DIM:
         return headed(queries, keys, values, random_blocks, global_blocks)
     return exchanged(queries, keys, values, random_blocks, global_blocks)

time: 38.8 us -> 36 us (0.928)
  the two profiles are of different devices: /device:TPU:24 before, /device:TPU:1 now
where the time goes in v2:
time: 36 us; the launch traced here: 35.8 us
  Pallas kernels  35 us (97%)
  other arithmetic  0.85 us (2%)
    pallas_call x1, Pallas kernels, headed(): pl.pallas_call(functools.partial(headed_kernel, seq_count, head_count, ra...  35 us
    convert_element_type x1, other arithmetic, headed(): return result.astype(jnp.float32)  0.85 us

profile of v2, /device:TPU:1, one launch (start us, length us, event | category | flops | bytes accessed | tf_op | source)
XLA Modules:
  0.0 35.8 jit_solution(5479987526466475954)
XLA Ops:
  0.0 35.0 %shard_map.55 = bf16[256,512]{1,0:T(8,128)(2,1)S(1)} custom-call(bf16[64,2048]{1,0:T(8,128)(2,1)} %q_hbm.1, bf16[64,2048]{1,0:T(8,128)(2,1)} %k_hbm.1, bf16[64,2048]{1,0:T(8,128)(2,1)} %v_hbm.1, s32[3,4,4]{2,1,0:T(4,128)} %bitcast.1, s32[2]{0:T(128)} %glob_ref.1), custom_call_target="tpu_custom_call" | custom-call | tf_op jit(solution)/shard_map/pallas_call | solution.py:491
  35.0 0.9 %convert_element_type.3 = f32[256,512]{1,0:T(8,128)} convert(bf16[256,512]{1,0:T(8,128)(2,1)S(1)} %shard_map.55) | non-fusion elementwise | flops 131072 | bytes 786432 | tf_op jit(solution)/shard_map/convert_element_type | solution.py:527

commit v3 on v2

--- a/solution.py
+++ b/solution.py
@@ -193,7 +193,7 @@
     seq_count, head_count, rand_count,
     q_hbm, k_hbm, v_hbm, rand_hbm, glob_ref, out_ref,
     k_pool, v_pool, q_early, q_late, rand_own, rand_tile, rand_vmem, rand_smem, p_buf, tot_buf, full_p, full_tot,
-    full_out, o_buf, local_sem, send_sem, pass_sem, rand_send, o_send,
+    full_out, o_buf, local_sem, go_sem, send_sem, pass_sem, rand_send, o_send,
     k_sem, v_sem, q_sem, o_sem, rand_sem,
 ):
     seq = lax.axis_index("seq")
@@ -231,16 +231,23 @@
     def leave(piece, sender):
         remote(piece, piece, sender, local_sem.at[0], partner).wait_send()
 
+    half = depth // 2
+    middle = (z == half - 1) | (z == half)
+    across = jnp.where(z < half, seq + 2, seq - 2)
     barrier = pltpu.get_barrier_semaphore()
-    friends = 0
-    for ds in range(seq_count):
-        for dh in range(head_count):
-            if ds or dh:
-                friend = {"seq": (seq + ds) % seq_count, "head": (head + dh) % head_count}
-                pl.semaphore_signal(
-                    barrier, inc=1, device_id=friend, device_id_type=pl.DeviceIdType.MESH
+
+    def signal(semaphore, target):
+        pl.semaphore_signal(
+            semaphore, inc=1, device_id=target, device_id_type=pl.DeviceIdType.MESH
+        )
+
+    for there in range(seq_count):
+        if there // 2 not in (half - 1, half):
+            for twin in range(head_count):
+                pl.when((seq != there) | (head != twin))(
+                    lambda there=there, twin=twin: signal(barrier, {"seq": there, "head": twin})
                 )
-                friends += 1
+    pl.when(middle)(lambda: signal(barrier, {"seq": across, "head": head}))
 
     def columns(there, lane):
         return pl.ds(pl.multiple_of((lane * seq_count + there) * HEAD_DIM, HEAD_DIM), HEAD_DIM)
@@ -265,9 +272,30 @@
     own_names.wait()
     for r in range(rand_count):
         rand_tile[:head_count, r * heads_dev : (r + 1) * heads_dev] = rand_own[r]
-    pl.semaphore_wait(barrier, friends)
-
-    steps = list(range(1, depth)) + [0]
+
+    def first_across():
+        pl.semaphore_wait(barrier, 1)
+        step = jnp.where(z < half, 1, depth - 1)
+        for kind, source, dest, receiver in (
+            (0, k_hbm, k_pool.at[mine + 1], k_sem.at[mine]),
+            (1, v_hbm, v_pool.at[mine + 1], v_sem.at[mine]),
+            (2, q_hbm, q_early.at[seq * early_lanes], q_sem.at[slot]),
+        ):
+            remote(
+                source.at[:, columns(across, x)], dest, send_sem.at[kind, step * 2 * lanes],
+                receiver, device(across, x),
+            ).start()
+        pl.semaphore_wait(go_sem, 1)
+
+    def all_here():
+        pl.semaphore_wait(barrier, seq_count * head_count - 1)
+        beside = (z == half - 2) | (z == half + 1)
+        pl.when(beside)(lambda: signal(go_sem, {"seq": across, "head": head}))
+
+    pl.when(middle)(first_across)
+    pl.when(jnp.logical_not(middle))(all_here)
+
+    steps = [depth - 1] + list(range(1, depth - 1)) + [0]
 
     def push(kind, source, dest, receiver, lane_steps):
         for step in steps:
@@ -276,10 +304,15 @@
                     if step or dy or dx:
                         there, lane = 2 * ((z + step) % depth) + (y + dy) % 2, (x + dx) % lanes
                         sender = send_sem.at[kind, (step * 2 + dy) * lanes + dx]
-                        remote(
+                        copy = remote(
                             source.at[:, columns(there, lane)], dest(dx), sender, receiver,
                             device(there, lane),
-                        ).start()
+                        )
+                        if dy or dx or not step:
+                            copy.start()
+                        else:
+                            done = middle & (there == across)
+                            pl.when(jnp.logical_not(done))(lambda copy=copy: copy.start())
 
     def post_or_keep(source, dest, sender, receiver, target, at_home):
         copy = remote(source, dest, sender, receiver, target)
@@ -510,6 +543,7 @@
             f32(2 * BLK, HEAD_DIM),
             bf16(span, *tile),
             dma((2,)),
+            pltpu.SemaphoreType.REGULAR,
             dma((3, span)),
             dma((2, span)),
             dma((heads_dev + 1,)),
@@ -532,7 +566,7 @@
     rows, width = queries.shape
     span = seq_count * head_count // 2
     fits = 6 * rows * width * span // head_count <= POOL_LIMIT
-    even = seq_count % 2 == 0 and head_count % 2 == 0 and global_blocks.shape[0] == 2
+    even = seq_count % 4 == 0 and seq_count > 4 and head_count % 2 == 0 and global_blocks.shape[0] == 2
     if fits and even and rows == BLK and width == span * HEAD_DIM:
         return headed(queries, keys, values, random_blocks, global_blocks)
     return exchanged(queries, keys, values, random_blocks, global_blocks)

time: 36 us -> 35.8 us (level)
  no operation moved by 1% of the time
where the time goes in v3:
time: 35.8 us; the launch traced here: 35.7 us
  Pallas kernels  34.8 us (97%)
  other arithmetic  0.85 us (2%)
    pallas_call x1, Pallas kernels, headed(): pl.pallas_call(functools.partial(headed_kernel, seq_count, head_count, ra...  34.8 us
    convert_element_type x1, other arithmetic, headed(): return result.astype(jnp.float32)  0.85 us

profile of v3, /device:TPU:1, one launch (start us, length us, event | category | flops | bytes accessed | tf_op | source)
XLA Modules:
  0.0 35.7 jit_solution(8089507324339581098)
XLA Ops:
  0.0 34.8 %shard_map.55 = bf16[256,512]{1,0:T(8,128)(2,1)S(1)} custom-call(bf16[64,2048]{1,0:T(8,128)(2,1)} %q_hbm.1, bf16[64,2048]{1,0:T(8,128)(2,1)} %k_hbm.1, bf16[64,2048]{1,0:T(8,128)(2,1)} %v_hbm.1, s32[3,4,4]{2,1,0:T(4,128)} %bitcast.1, s32[2]{0:T(128)} %glob_ref.1), custom_call_target="tpu_custom_call" | custom-call | tf_op jit(solution)/shard_map/pallas_call | solution.py:524
  34.8 0.9 %convert_element_type.3 = f32[256,512]{1,0:T(8,128)} convert(bf16[256,512]{1,0:T(8,128)(2,1)S(1)} %shard_map.55) | non-fusion elementwise | flops 131072 | bytes 786432 | tf_op jit(solution)/shard_map/convert_element_type | solution.py:561
